TPU v7x, 32 devices: a whole 2x2x4 slice. The times are simulated.
32 devices in a mesh: layer: 2 (over core), row: 4 (over y, x), col: 4 (over z).
Axes of the slice: x: 2, y: 2, z: 4, core: 2. Of those that a mesh axis runs over, the one named last changes fastest.
Arguments:
- root_rhs: float32 [32, 8, 1024], P(None, None, 'row'), may hold values from -6 to 6
- child_rhs: float32 [2, 32, 8, 1024], P('layer', None, None, 'row'), may hold values from -6 to 6
- root_factor: float32 [8, 8, 1024, 1024], P(None, None, 'row', 'col'), may hold values from -0.0625 to 0.0625
- child_factor: float32 [2, 8, 8, 1024, 1024], P('layer', None, None, 'row', 'col'), may hold values from -0.0625 to 0.0625
- coupling: float32 [2, 8, 8, 1024, 1024], P('layer', None, None, 'row', 'col'), may hold values from -0.0234375 to 0.0234375
- root_inverse: float32 [8, 1024, 1024], P(None, 'col', 'row'), as said below
- child_inverse: float32 [2, 8, 1024, 1024], P('layer', None, 'col', 'row'), as said below
Outputs:
- root_solution: float32 [32, 8, 1024], P(None, None, 'row')
- child_solution: float32 [2, 32, 8, 1024], P('layer', None, None, 'row')
Inputs may be any that keep to these rules, and one draw needn't show every extreme that they name: Each block of root_inverse is lower triangular. Each block of child_inverse is lower triangular.
All inputs are finite; a program needn't handle non-finite values.
Results may differ from a plain program's by a relative error of at most 0.00015.
Values sent between devices are 32-bit elements; how exact they have to be, the bound alone decides.
No kernel may reach another device: no remote copies, remote signals or barrier semaphores. Data moves between devices by JAX's collectives and lax.ppermute only.
A program may use at most 128 MiB of HBM per device.

v0:
```python
import jax
import jax.numpy as jnp
from jax import lax
from jax.sharding import PartitionSpec as P

precise = lax.Precision.HIGHEST


def pick(stack, index, axis):
    return lax.dynamic_index_in_dim(stack, index, axis, keepdims=False)


def forward(factor, inverse, right, extra, first_col):
    blocks = factor.shape[0]
    columns = right.shape[0]
    col_width = factor.shape[3]
    right_rows = jnp.transpose(right, (1, 0, 2))
    solved = jnp.zeros((blocks, columns, col_width), jnp.float32)

    def forward_step(target, solved):
        row_tiles = pick(factor, target, 0)
        partial_value = jnp.where(first_col, pick(right_rows, target, 0), 0.0) - pick(
            extra, target, 0
        )
        partial_value = partial_value - jnp.einsum(
            "jna,jba->nb", solved, row_tiles, precision=precise
        )
        residual = lax.psum(partial_value, "col")
        share = jnp.einsum("nb,ab->na", residual, pick(inverse, target, 0), precision=precise)
        solved_block = lax.psum(share, "row")
        return lax.dynamic_update_index_in_dim(solved, solved_block, target, 0)

    return lax.fori_loop(0, blocks, forward_step, solved)


def backward(factor, inverse, values, lowered, first_row):
    blocks = factor.shape[0]
    columns = values.shape[1]
    row_width = factor.shape[2]
    solved = jnp.zeros((blocks, columns, row_width), jnp.float32)

    def backward_step(step_at, solved):
        target = blocks - 1 - step_at
        column_tiles = pick(factor, target, 1)
        partial_value = jnp.where(first_row, pick(values, target, 0), 0.0) - pick(
            lowered, target, 0
        )
        partial_value = partial_value - jnp.einsum(
            "inb,iba->na", solved, column_tiles, precision=precise
        )
        pending = lax.psum(partial_value, "row")
        share = jnp.einsum("na,ab->nb", pending, pick(inverse, target, 0), precision=precise)
        solved_block = lax.psum(share, "col")
        return lax.dynamic_update_index_in_dim(solved, solved_block, target, 0)

    return lax.fori_loop(0, blocks, backward_step, solved)


def local(root_rhs, child_rhs, root_factor, child_factor, coupling, root_inverse, child_inverse):
    first_row = lax.axis_index("row") == 0
    first_col = lax.axis_index("col") == 0
    columns = root_rhs.shape[0]
    child_blocks = child_factor[0]
    child_inverses = child_inverse[0]
    couple_blocks = coupling[0]
    child_count = child_blocks.shape[0]
    root_count = root_factor.shape[0]
    row_width = root_factor.shape[2]
    col_width = root_factor.shape[3]
    child_down, root_down = (child_inverses, root_inverse)
    child_up, root_up = (child_inverses, root_inverse)
    child_start = jnp.zeros((child_count, columns, row_width), jnp.float32)
    child_forward = forward(child_blocks, child_down, child_rhs[0], child_start, first_col)
    lifted = jnp.einsum("jna,kjba->knb", child_forward, couple_blocks, precision=precise)
    lifted = lax.psum_scatter(lifted, "layer", scatter_dimension=1, tiled=True)
    half_cols = lifted.shape[1]
    layer_index = lax.axis_index("layer")
    right_half = lax.dynamic_slice_in_dim(root_rhs, layer_index * half_cols, half_cols, 0)
    root_forward = forward(root_factor, root_down, right_half, lifted, first_col)
    empty = jnp.zeros((root_count, half_cols, col_width), jnp.float32)
    root_half = backward(root_factor, root_up, root_forward, empty, first_row)
    root_solved = lax.all_gather(root_half, "layer", axis=1, tiled=True)
    lowered = jnp.einsum("inb,ikba->kna", root_solved, couple_blocks, precision=precise)
    child_solved = backward(child_blocks, child_up, child_forward, lowered, first_row)
    root_solution = jnp.transpose(root_solved, (1, 0, 2))
    child_solution = jnp.transpose(child_solved, (1, 0, 2))[None]
    return (root_solution, child_solution)


def solution(mesh):
    in_specs = (
        P(None, None, "row"),
        P("layer", None, None, "row"),
        P(None, None, "row", "col"),
        P("layer", None, None, "row", "col"),
        P("layer", None, None, "row", "col"),
        P(None, "col", "row"),
        P("layer", None, "col", "row"),
    )
    out_specs = (P(None, None, "row"), P("layer", None, None, "row"))
    return jax.shard_map(local, mesh=mesh, in_specs=in_specs, out_specs=out_specs, check_vma=False)
```

profile of v0, /device:TPU:0, one launch (start us, length us, event | category | flops | bytes accessed | tf_op | source)
XLA Modules:
  0.0 1199.0 jit_solution(10742382642102309621)
XLA Ops:
  8.3 295.6 %while.56 = (s32[]{:T(128)}, f32[8,32,256]{2,1,0:T(8,128)S(1)}, pred[]{:T(512)}, f32[8,32,256]{2,1,0:T(8,128)S(1)}, f32[8,8,256,256]{3,2,1,0:T(8,128)}, /*index=5*/f32[8,256,256]{2,1,0:T(8,128)}, s32[]{:T(128)}) while((s32[]{:T(128)}, f32[8,32,256]{2,1,0:T(8,128)S(1)}, pred[]{:T(512)}, f32[8,32,256]{2,1,0:T(8,128)S(1)}, ...), condition=%wide.region_3.4_spmd, body=%wide.region_0.3_spmd.sunk | while | flops 226525184 | bytes 2950749 | solution.py:33
  11.8 20.9 %psum.108 = f32[32,256]{1,0:T(8,128)S(1)} all-reduce(f32[32,256]{1,0:T(8,128)S(1)} %fusion.96), channel_id=1, replica_groups=mesh['layer'=2,'row'=4,'col'=4] {'col'}, use_global_device_ids=true, to_apply=%region_1.1 | all-reduce | flops 8192 | bytes 65536 | tf_op jit(solution)/shard_map/while/body/eval_jaxpr/psum | solution.py:28
  34.0 16.3 %psum.109 = f32[1,32,256]{2,1,0:T(8,128)S(1)} all-reduce(f32[1,32,256]{2,1,0:T(8,128)S(1)} %convolution_bitcast_fusion.8), channel_id=1, replica_groups=mesh['layer'=2,'row'=4,'col'=4] {'row'}, use_global_device_ids=true, to_apply=%region_2.2 | all-reduce | flops 8192 | bytes 65536 | tf_op jit(solution)/shard_map/while/body/eval_jaxpr/psum | solution.py:30
  53.8 15.8 %psum.108 = f32[32,256]{1,0:T(8,128)S(1)} all-reduce(f32[32,256]{1,0:T(8,128)S(1)} %fusion.96), channel_id=1, replica_groups=mesh['layer'=2,'row'=4,'col'=4] {'col'}, use_global_device_ids=true, to_apply=%region_1.1 | all-reduce | flops 8192 | bytes 65536 | tf_op jit(solution)/shard_map/while/body/eval_jaxpr/psum | solution.py:28
  88.6 17.5 %psum.108 = f32[32,256]{1,0:T(8,128)S(1)} all-reduce(f32[32,256]{1,0:T(8,128)S(1)} %fusion.96), channel_id=1, replica_groups=mesh['layer'=2,'row'=4,'col'=4] {'col'}, use_global_device_ids=true, to_apply=%region_1.1 | all-reduce | flops 8192 | bytes 65536 | tf_op jit(solution)/shard_map/while/body/eval_jaxpr/psum | solution.py:28
  126.5 15.8 %psum.108 = f32[32,256]{1,0:T(8,128)S(1)} all-reduce(f32[32,256]{1,0:T(8,128)S(1)} %fusion.96), channel_id=1, replica_groups=mesh['layer'=2,'row'=4,'col'=4] {'col'}, use_global_device_ids=true, to_apply=%region_1.1 | all-reduce | flops 8192 | bytes 65536 | tf_op jit(solution)/shard_map/while/body/eval_jaxpr/psum | solution.py:28
  161.3 17.5 %psum.108 = f32[32,256]{1,0:T(8,128)S(1)} all-reduce(f32[32,256]{1,0:T(8,128)S(1)} %fusion.96), channel_id=1, replica_groups=mesh['layer'=2,'row'=4,'col'=4] {'col'}, use_global_device_ids=true, to_apply=%region_1.1 | all-reduce | flops 8192 | bytes 65536 | tf_op jit(solution)/shard_map/while/body/eval_jaxpr/psum | solution.py:28
  180.1 16.3 %psum.109 = f32[1,32,256]{2,1,0:T(8,128)S(1)} all-reduce(f32[1,32,256]{2,1,0:T(8,128)S(1)} %convolution_bitcast_fusion.8), channel_id=1, replica_groups=mesh['layer'=2,'row'=4,'col'=4] {'row'}, use_global_device_ids=true, to_apply=%region_2.2 | all-reduce | flops 8192 | bytes 65536 | tf_op jit(solution)/shard_map/while/body/eval_jaxpr/psum | solution.py:30
  199.9 15.8 %psum.108 = f32[32,256]{1,0:T(8,128)S(1)} all-reduce(f32[32,256]{1,0:T(8,128)S(1)} %fusion.96), channel_id=1, replica_groups=mesh['layer'=2,'row'=4,'col'=4] {'col'}, use_global_device_ids=true, to_apply=%region_1.1 | all-reduce | flops 8192 | bytes 65536 | tf_op jit(solution)/shard_map/while/body/eval_jaxpr/psum | solution.py:28
  234.8 17.4 %psum.108 = f32[32,256]{1,0:T(8,128)S(1)} all-reduce(f32[32,256]{1,0:T(8,128)S(1)} %fusion.96), channel_id=1, replica_groups=mesh['layer'=2,'row'=4,'col'=4] {'col'}, use_global_device_ids=true, to_apply=%region_1.1 | all-reduce | flops 8192 | bytes 65536 | tf_op jit(solution)/shard_map/while/body/eval_jaxpr/psum | solution.py:28
  272.6 15.8 %psum.108 = f32[32,256]{1,0:T(8,128)S(1)} all-reduce(f32[32,256]{1,0:T(8,128)S(1)} %fusion.96), channel_id=1, replica_groups=mesh['layer'=2,'row'=4,'col'=4] {'col'}, use_global_device_ids=true, to_apply=%region_1.1 | all-reduce | flops 8192 | bytes 65536 | tf_op jit(solution)/shard_map/while/body/eval_jaxpr/psum | solution.py:28
  303.9 19.2 %fusion.56 = f32[8,32,256]{2,1,0:T(8,128)} fusion(f32[1,8,8,256,256]{4,3,2,1,0:T(8,128)} %param.19, f32[8,32,256]{2,1,0:T(8,128)S(1)} %get-tuple-element.861), kind=kOutput, calls=%fused_computation.48 | convolution fusion | flops 1610612736 | bytes 17301504 | tf_op jit(solution)/shard_map/jna,kjba->knb/dot_general | solution.py:74
  330.4 284.1 %while.57 = (s32[]{:T(128)}, f32[8,16,256]{2,1,0:T(8,128)S(1)}, pred[]{:T(512)}, f32[8,16,256]{2,1,0:T(8,128)S(1)}, f32[8,16,256]{2,1,0:T(8,128)}, /*index=5*/f3...) while((s32[]{:T(128)}, f32[8,16,256]{2,1,0:T(8,128)S(1)}, pred[]{:T(512)}, ...), condition=%wide.region_8.9_spmd, body=%wide.region_5.8_spmd.sunk | while | flops 113266688 | bytes 2672229 | solution.py:33
  333.7 18.9 %psum.110 = f32[16,256]{1,0:T(8,128)S(1)} all-reduce(f32[16,256]{1,0:T(8,128)S(1)} %fusion.101), channel_id=1, replica_groups=mesh['layer'=2,'row'=4,'col'=4] {'col'}, use_global_device_ids=true, to_apply=%region_6.6 | all-reduce | flops 4096 | bytes 32768 | tf_op jit(solution)/shard_map/while/body/eval_jaxpr/psum | solution.py:28
  353.9 16.1 %psum.111 = f32[1,16,256]{2,1,0:T(8,128)S(1)} all-reduce(f32[1,16,256]{2,1,0:T(8,128)S(1)} %convolution_bitcast_fusion.9), channel_id=1, replica_groups=mesh['layer'=2,'row'=4,'col'=4] {'row'}, use_global_device_ids=true, to_apply=%region_7.7 | all-reduce | flops 4096 | bytes 32768 | tf_op jit(solution)/shard_map/while/body/eval_jaxpr/psum | solution.py:30
  407.2 16.3 %psum.110 = f32[16,256]{1,0:T(8,128)S(1)} all-reduce(f32[16,256]{1,0:T(8,128)S(1)} %fusion.101), channel_id=1, replica_groups=mesh['layer'=2,'row'=4,'col'=4] {'col'}, use_global_device_ids=true, to_apply=%region_6.6 | all-reduce | flops 4096 | bytes 32768 | tf_op jit(solution)/shard_map/while/body/eval_jaxpr/psum | solution.py:28
  477.4 16.3 %psum.110 = f32[16,256]{1,0:T(8,128)S(1)} all-reduce(f32[16,256]{1,0:T(8,128)S(1)} %fusion.101), channel_id=1, replica_groups=mesh['layer'=2,'row'=4,'col'=4] {'col'}, use_global_device_ids=true, to_apply=%region_6.6 | all-reduce | flops 4096 | bytes 32768 | tf_op jit(solution)/shard_map/while/body/eval_jaxpr/psum | solution.py:28
  547.6 16.3 %psum.110 = f32[16,256]{1,0:T(8,128)S(1)} all-reduce(f32[16,256]{1,0:T(8,128)S(1)} %fusion.101), channel_id=1, replica_groups=mesh['layer'=2,'row'=4,'col'=4] {'col'}, use_global_device_ids=true, to_apply=%region_6.6 | all-reduce | flops 4096 | bytes 32768 | tf_op jit(solution)/shard_map/while/body/eval_jaxpr/psum | solution.py:28
  614.5 274.9 %while.58 = (s32[]{:T(128)}, f32[8,16,256]{2,1,0:T(8,128)S(1)}, pred[]{:T(512)}, f32[8,16,256]{2,1,0:T(8,128)S(1)}, f32[8,8,256,256]{3,2,1,0:T(8,128)}, /*index=...) while((s32[]{:T(128)}, f32[8,16,256]{2,1,0:T(8,128)S(1)}, pred[]{:T(512)}, ...), condition=%wide.region_12.13_spmd, body=%wide.region_9.12_spmd.sunk | while | flops 113262600 | bytes 2655907 | solution.py:56
  633.8 16.3 %psum.113 = f32[1,16,256]{2,1,0:T(8,128)S(1)} all-reduce(f32[1,16,256]{2,1,0:T(8,128)S(1)} %convolution_bitcast_fusion.10), channel_id=1, replica_groups=mesh['layer'=2,'row'=4,'col'=4] {'col'}, use_global_device_ids=true, to_apply=%region_11.11 | all-reduce | flops 4096 | bytes 32768 | tf_op jit(solution)/shard_map/while/body/eval_jaxpr/psum | solution.py:53
  702.5 16.2 %psum.113 = f32[1,16,256]{2,1,0:T(8,128)S(1)} all-reduce(f32[1,16,256]{2,1,0:T(8,128)S(1)} %convolution_bitcast_fusion.10), channel_id=1, replica_groups=mesh['layer'=2,'row'=4,'col'=4] {'col'}, use_global_device_ids=true, to_apply=%region_11.11 | all-reduce | flops 4096 | bytes 32768 | tf_op jit(solution)/shard_map/while/body/eval_jaxpr/psum | solution.py:53
  771.2 16.3 %psum.113 = f32[1,16,256]{2,1,0:T(8,128)S(1)} all-reduce(f32[1,16,256]{2,1,0:T(8,128)S(1)} %convolution_bitcast_fusion.10), channel_id=1, replica_groups=mesh['layer'=2,'row'=4,'col'=4] {'col'}, use_global_device_ids=true, to_apply=%region_11.11 | all-reduce | flops 4096 | bytes 32768 | tf_op jit(solution)/shard_map/while/body/eval_jaxpr/psum | solution.py:53
  839.9 16.3 %psum.113 = f32[1,16,256]{2,1,0:T(8,128)S(1)} all-reduce(f32[1,16,256]{2,1,0:T(8,128)S(1)} %convolution_bitcast_fusion.10), channel_id=1, replica_groups=mesh['layer'=2,'row'=4,'col'=4] {'col'}, use_global_device_ids=true, to_apply=%region_11.11 | all-reduce | flops 4096 | bytes 32768 | tf_op jit(solution)/shard_map/while/body/eval_jaxpr/psum | solution.py:53
  905.6 285.7 %while.59 = (s32[]{:T(128)}, f32[8,32,256]{2,1,0:T(8,128)S(1)}, pred[]{:T(512)}, f32[8,32,256]{2,1,0:T(8,128)S(1)}, f32[8,32,256]{2,1,0:T(8,128)S(1)}, /*index=5...) while((s32[]{:T(128)}, f32[8,32,256]{2,1,0:T(8,128)S(1)}, ...), condition=%wide.region_16.17_spmd, body=%wide.region_13.16_spmd.sunk | while | flops 226533376 | bytes 2983595 | solution.py:56
  925.2 16.6 %psum.115 = f32[1,32,256]{2,1,0:T(8,128)S(1)} all-reduce(f32[1,32,256]{2,1,0:T(8,128)S(1)} %convolution_bitcast_fusion.11), channel_id=1, replica_groups=mesh['layer'=2,'row'=4,'col'=4] {'col'}, use_global_device_ids=true, to_apply=%region_15.15 | all-reduce | flops 8192 | bytes 65536 | tf_op jit(solution)/shard_map/while/body/eval_jaxpr/psum | solution.py:53
  960.0 16.7 %psum.115 = f32[1,32,256]{2,1,0:T(8,128)S(1)} all-reduce(f32[1,32,256]{2,1,0:T(8,128)S(1)} %convolution_bitcast_fusion.11), channel_id=1, replica_groups=mesh['layer'=2,'row'=4,'col'=4] {'col'}, use_global_device_ids=true, to_apply=%region_15.15 | all-reduce | flops 8192 | bytes 65536 | tf_op jit(solution)/shard_map/while/body/eval_jaxpr/psum | solution.py:53
  996.2 16.6 %psum.115 = f32[1,32,256]{2,1,0:T(8,128)S(1)} all-reduce(f32[1,32,256]{2,1,0:T(8,128)S(1)} %convolution_bitcast_fusion.11), channel_id=1, replica_groups=mesh['layer'=2,'row'=4,'col'=4] {'col'}, use_global_device_ids=true, to_apply=%region_15.15 | all-reduce | flops 8192 | bytes 65536 | tf_op jit(solution)/shard_map/while/body/eval_jaxpr/psum | solution.py:53
  1031.6 16.9 %psum.115 = f32[1,32,256]{2,1,0:T(8,128)S(1)} all-reduce(f32[1,32,256]{2,1,0:T(8,128)S(1)} %convolution_bitcast_fusion.11), channel_id=1, replica_groups=mesh['layer'=2,'row'=4,'col'=4] {'col'}, use_global_device_ids=true, to_apply=%region_15.15 | all-reduce | flops 8192 | bytes 65536 | tf_op jit(solution)/shard_map/while/body/eval_jaxpr/psum | solution.py:53
  1068.0 16.7 %psum.115 = f32[1,32,256]{2,1,0:T(8,128)S(1)} all-reduce(f32[1,32,256]{2,1,0:T(8,128)S(1)} %convolution_bitcast_fusion.11), channel_id=1, replica_groups=mesh['layer'=2,'row'=4,'col'=4] {'col'}, use_global_device_ids=true, to_apply=%region_15.15 | all-reduce | flops 8192 | bytes 65536 | tf_op jit(solution)/shard_map/while/body/eval_jaxpr/psum | solution.py:53
  1103.0 16.7 %psum.115 = f32[1,32,256]{2,1,0:T(8,128)S(1)} all-reduce(f32[1,32,256]{2,1,0:T(8,128)S(1)} %convolution_bitcast_fusion.11), channel_id=1, replica_groups=mesh['layer'=2,'row'=4,'col'=4] {'col'}, use_global_device_ids=true, to_apply=%region_15.15 | all-reduce | flops 8192 | bytes 65536 | tf_op jit(solution)/shard_map/while/body/eval_jaxpr/psum | solution.py:53
  1139.1 16.6 %psum.115 = f32[1,32,256]{2,1,0:T(8,128)S(1)} all-reduce(f32[1,32,256]{2,1,0:T(8,128)S(1)} %convolution_bitcast_fusion.11), channel_id=1, replica_groups=mesh['layer'=2,'row'=4,'col'=4] {'col'}, use_global_device_ids=true, to_apply=%region_15.15 | all-reduce | flops 8192 | bytes 65536 | tf_op jit(solution)/shard_map/while/body/eval_jaxpr/psum | solution.py:53
  1174.3 16.9 %psum.115 = f32[1,32,256]{2,1,0:T(8,128)S(1)} all-reduce(f32[1,32,256]{2,1,0:T(8,128)S(1)} %convolution_bitcast_fusion.11), channel_id=1, replica_groups=mesh['layer'=2,'row'=4,'col'=4] {'col'}, use_global_device_ids=true, to_apply=%region_15.15 | all-reduce | flops 8192 | bytes 65536 | tf_op jit(solution)/shard_map/while/body/eval_jaxpr/psum | solution.py:53
  (149 shorter events, 712.7 us)
Async XLA Ops:
  7.2 316.0 %copy-start = (f32[32,8,256]{2,1,0:T(8,128)S(1)}, f32[32,8,256]{2,1,0:T(8,128)}, u32[]{:S(2)}) copy-start(f32[32,8,256]{2,1,0:T(8,128)} %param.15) | copy-start | bytes 786436
  7.2 323.2 %reduce-scatter.2.cloned.1.call-start = ((), (), s32[]{:S(2)}) async-start(), calls=%async_computation.1 | async-start | bytes 393216 | tf_op jit(solution)/shard_map/reduce_scatter | solution.py:75
Sparse Core Ops, SparseCore 0:
  323.2 7.0 reduce-scatter.1
where the time goes:
time: 1200 us
  blocking collectives  1000 us (83%)
  matrix products  169 us (14%)
  between operations  14.1 us (1%)
    psum x16, blocking collectives, forward_step(): residual = lax.psum(partial_value, 'col')  266 us
    psum x16, blocking collectives, backward_step(): solved_block = lax.psum(share, 'col')  261 us
    psum x16, blocking collectives, forward_step(): solved_block = lax.psum(share, 'row')  238 us
    psum x16, blocking collectives, backward_step(): pending = lax.psum(partial_value, 'row')  236 us
    dot_general x16, matrix products, forward_step(): jnp.einsum('jna,jba->nb', solved, row_tiles, precision=precise)  54.5 us
    dot_general x16, matrix products, backward_step(): jnp.einsum('inb,iba->na', solved, column_tiles, precision=precise)  43.7 us
  transfers between devices with their start and end apart: 1, of which 1 were waited for; matrix products, arithmetic and copies ran while one was open for 0% of the time, Pallas kernels for 0%

commit v1 on v0

--- a/solution.py
+++ b/solution.py
@@ -4,6 +4,22 @@
 from jax.sharding import PartitionSpec as P
 
 precise = lax.Precision.HIGHEST
+
+
+def waves_compute(message):
+    mesh_ax = "col"
+    full_n = lax.axis_size(mesh_ax)
+
+    def remake_ticks(taken_in, reached):
+        if reached >= full_n:
+            return taken_in
+        lanes = []
+        for idx in range(full_n):
+            lanes.append((idx, idx ^ reached))
+        formed = lax.ppermute(taken_in, mesh_ax, lanes)
+        return remake_ticks(taken_in + formed, 2 * reached)
+
+    return remake_ticks(message, 1)
 
 
 def pick(stack, index, axis):
@@ -50,7 +66,7 @@
         )
         pending = lax.psum(partial_value, "row")
         share = jnp.einsum("na,ab->nb", pending, pick(inverse, target, 0), precision=precise)
-        solved_block = lax.psum(share, "col")
+        solved_block = waves_compute(share)
         return lax.dynamic_update_index_in_dim(solved, solved_block, target, 0)
 
     return lax.fori_loop(0, blocks, backward_step, solved)

time: 1200 us -> 1080 us (0.900)
  blocking collectives: 1000 us -> 743 us
  waiting for transfers between devices: 7.17 us -> 140 us
    psum x16 -> x0, blocking collectives: 261 us -> none  [backward_step(): solved_block = lax.psum(share, 'col')]
    ppermute x0 -> x32, waiting for transfers between devices: none -> 132 us  [remake_ticks(): formed = lax.ppermute(taken_in, mesh_ax, lanes)]
  transfers between devices with their start and end apart: 1 -> 33, of which waited for: 1 -> 33; matrix products, arithmetic and copies ran while one was open for 0% -> 0% of each run, Pallas kernels for 0% -> 0%
where the time goes in v1:
time: 1080 us
  blocking collectives  743 us (69%)
  matrix products  169 us (16%)
  waiting for transfers between devices  140 us (13%)
  between operations  14.1 us (1%)
    psum x16, blocking collectives, forward_step(): residual = lax.psum(partial_value, 'col')  266 us
    psum x16, blocking collectives, forward_step(): solved_block = lax.psum(share, 'row')  238 us
    psum x16, blocking collectives, backward_step(): pending = lax.psum(partial_value, 'row')  237 us
    ppermute x32, waiting for transfers between devices, remake_ticks(): formed = lax.ppermute(taken_in, mesh_ax, lanes)  132 us
    dot_general x16, matrix products, forward_step(): jnp.einsum('jna,jba->nb', solved, row_tiles, precision=precise)  54.5 us
    dot_general x16, matrix products, backward_step(): jnp.einsum('inb,iba->na', solved, column_tiles, precision=precise)  43.7 us
  transfers between devices with their start and end apart: 33, of which 33 were waited for; matrix products, arithmetic and copies ran while one was open for 0% of the time, Pallas kernels for 0%

profile of v1, /device:TPU:0, one launch (start us, length us, event | category | flops | bytes accessed | tf_op | source)
XLA Modules:
  0.0 1076.1 jit_solution(8900188943634942839)
XLA Ops:
  8.3 295.6 %while.56 = (s32[]{:T(128)}, f32[8,32,256]{2,1,0:T(8,128)S(1)}, pred[]{:T(512)}, f32[8,32,256]{2,1,0:T(8,128)S(1)}, f32[8,8,256,256]{3,2,1,0:T(8,128)}, /*index=5*/f32[8,256,256]{2,1,0:T(8,128)}, s32[]{:T(128)}) while((s32[]{:T(128)}, f32[8,32,256]{2,1,0:T(8,128)S(1)}, pred[]{:T(512)}, f32[8,32,256]{2,1,0:T(8,128)S(1)}, ...), condition=%wide.region_3.4_spmd, body=%wide.region_0.3_spmd.sunk | while | flops 226525184 | bytes 2950749 | solution.py:49
  11.8 20.9 %psum.78 = f32[32,256]{1,0:T(8,128)S(1)} all-reduce(f32[32,256]{1,0:T(8,128)S(1)} %fusion.100), channel_id=1, replica_groups=mesh['layer'=2,'row'=4,'col'=4] {'col'}, use_global_device_ids=true, to_apply=%region_1.1 | all-reduce | flops 8192 | bytes 65536 | tf_op jit(solution)/shard_map/while/body/eval_jaxpr/psum | solution.py:44
  34.0 16.3 %psum.79 = f32[1,32,256]{2,1,0:T(8,128)S(1)} all-reduce(f32[1,32,256]{2,1,0:T(8,128)S(1)} %convolution_bitcast_fusion.4), channel_id=1, replica_groups=mesh['layer'=2,'row'=4,'col'=4] {'row'}, use_global_device_ids=true, to_apply=%region_2.2 | all-reduce | flops 8192 | bytes 65536 | tf_op jit(solution)/shard_map/while/body/eval_jaxpr/psum | solution.py:46
  53.8 15.8 %psum.78 = f32[32,256]{1,0:T(8,128)S(1)} all-reduce(f32[32,256]{1,0:T(8,128)S(1)} %fusion.100), channel_id=1, replica_groups=mesh['layer'=2,'row'=4,'col'=4] {'col'}, use_global_device_ids=true, to_apply=%region_1.1 | all-reduce | flops 8192 | bytes 65536 | tf_op jit(solution)/shard_map/while/body/eval_jaxpr/psum | solution.py:44
  88.6 17.5 %psum.78 = f32[32,256]{1,0:T(8,128)S(1)} all-reduce(f32[32,256]{1,0:T(8,128)S(1)} %fusion.100), channel_id=1, replica_groups=mesh['layer'=2,'row'=4,'col'=4] {'col'}, use_global_device_ids=true, to_apply=%region_1.1 | all-reduce | flops 8192 | bytes 65536 | tf_op jit(solution)/shard_map/while/body/eval_jaxpr/psum | solution.py:44
  107.5 15.6 %psum.79 = f32[1,32,256]{2,1,0:T(8,128)S(1)} all-reduce(f32[1,32,256]{2,1,0:T(8,128)S(1)} %convolution_bitcast_fusion.4), channel_id=1, replica_groups=mesh['layer'=2,'row'=4,'col'=4] {'row'}, use_global_device_ids=true, to_apply=%region_2.2 | all-reduce | flops 8192 | bytes 65536 | tf_op jit(solution)/shard_map/while/body/eval_jaxpr/psum | solution.py:46
  126.5 15.8 %psum.78 = f32[32,256]{1,0:T(8,128)S(1)} all-reduce(f32[32,256]{1,0:T(8,128)S(1)} %fusion.100), channel_id=1, replica_groups=mesh['layer'=2,'row'=4,'col'=4] {'col'}, use_global_device_ids=true, to_apply=%region_1.1 | all-reduce | flops 8192 | bytes 65536 | tf_op jit(solution)/shard_map/while/body/eval_jaxpr/psum | solution.py:44
  161.3 17.5 %psum.78 = f32[32,256]{1,0:T(8,128)S(1)} all-reduce(f32[32,256]{1,0:T(8,128)S(1)} %fusion.100), channel_id=1, replica_groups=mesh['layer'=2,'row'=4,'col'=4] {'col'}, use_global_device_ids=true, to_apply=%region_1.1 | all-reduce | flops 8192 | bytes 65536 | tf_op jit(solution)/shard_map/while/body/eval_jaxpr/psum | solution.py:44
  180.1 16.3 %psum.79 = f32[1,32,256]{2,1,0:T(8,128)S(1)} all-reduce(f32[1,32,256]{2,1,0:T(8,128)S(1)} %convolution_bitcast_fusion.4), channel_id=1, replica_groups=mesh['layer'=2,'row'=4,'col'=4] {'row'}, use_global_device_ids=true, to_apply=%region_2.2 | all-reduce | flops 8192 | bytes 65536 | tf_op jit(solution)/shard_map/while/body/eval_jaxpr/psum | solution.py:46
  199.9 15.8 %psum.78 = f32[32,256]{1,0:T(8,128)S(1)} all-reduce(f32[32,256]{1,0:T(8,128)S(1)} %fusion.100), channel_id=1, replica_groups=mesh['layer'=2,'row'=4,'col'=4] {'col'}, use_global_device_ids=true, to_apply=%region_1.1 | all-reduce | flops 8192 | bytes 65536 | tf_op jit(solution)/shard_map/while/body/eval_jaxpr/psum | solution.py:44
  234.8 17.4 %psum.78 = f32[32,256]{1,0:T(8,128)S(1)} all-reduce(f32[32,256]{1,0:T(8,128)S(1)} %fusion.100), channel_id=1, replica_groups=mesh['layer'=2,'row'=4,'col'=4] {'col'}, use_global_device_ids=true, to_apply=%region_1.1 | all-reduce | flops 8192 | bytes 65536 | tf_op jit(solution)/shard_map/while/body/eval_jaxpr/psum | solution.py:44
  253.5 15.6 %psum.79 = f32[1,32,256]{2,1,0:T(8,128)S(1)} all-reduce(f32[1,32,256]{2,1,0:T(8,128)S(1)} %convolution_bitcast_fusion.4), channel_id=1, replica_groups=mesh['layer'=2,'row'=4,'col'=4] {'row'}, use_global_device_ids=true, to_apply=%region_2.2 | all-reduce | flops 8192 | bytes 65536 | tf_op jit(solution)/shard_map/while/body/eval_jaxpr/psum | solution.py:46
  272.6 15.8 %psum.78 = f32[32,256]{1,0:T(8,128)S(1)} all-reduce(f32[32,256]{1,0:T(8,128)S(1)} %fusion.100), channel_id=1, replica_groups=mesh['layer'=2,'row'=4,'col'=4] {'col'}, use_global_device_ids=true, to_apply=%region_1.1 | all-reduce | flops 8192 | bytes 65536 | tf_op jit(solution)/shard_map/while/body/eval_jaxpr/psum | solution.py:44
  303.9 19.2 %fusion.58 = f32[8,32,256]{2,1,0:T(8,128)} fusion(f32[1,8,8,256,256]{4,3,2,1,0:T(8,128)} %param.19, f32[8,32,256]{2,1,0:T(8,128)S(1)} %get-tuple-element.861), kind=kOutput, calls=%fused_computation.48 | convolution fusion | flops 1610612736 | bytes 17301504 | tf_op jit(solution)/shard_map/jna,kjba->knb/dot_general | solution.py:90
  330.4 284.1 %while.57 = (s32[]{:T(128)}, f32[8,16,256]{2,1,0:T(8,128)S(1)}, pred[]{:T(512)}, f32[8,16,256]{2,1,0:T(8,128)S(1)}, f32[8,16,256]{2,1,0:T(8,128)}, /*index=5*/f3...) while((s32[]{:T(128)}, f32[8,16,256]{2,1,0:T(8,128)S(1)}, pred[]{:T(512)}, ...), condition=%wide.region_8.9_spmd, body=%wide.region_5.8_spmd.sunk | while | flops 113266688 | bytes 2672229 | solution.py:49
  333.7 18.9 %psum.80 = f32[16,256]{1,0:T(8,128)S(1)} all-reduce(f32[16,256]{1,0:T(8,128)S(1)} %fusion.105), channel_id=1, replica_groups=mesh['layer'=2,'row'=4,'col'=4] {'col'}, use_global_device_ids=true, to_apply=%region_6.6 | all-reduce | flops 4096 | bytes 32768 | tf_op jit(solution)/shard_map/while/body/eval_jaxpr/psum | solution.py:44
  353.9 16.1 %psum.81 = f32[1,16,256]{2,1,0:T(8,128)S(1)} all-reduce(f32[1,16,256]{2,1,0:T(8,128)S(1)} %convolution_bitcast_fusion.5), channel_id=1, replica_groups=mesh['layer'=2,'row'=4,'col'=4] {'row'}, use_global_device_ids=true, to_apply=%region_7.7 | all-reduce | flops 4096 | bytes 32768 | tf_op jit(solution)/shard_map/while/body/eval_jaxpr/psum | solution.py:46
  373.3 15.6 %psum.80 = f32[16,256]{1,0:T(8,128)S(1)} all-reduce(f32[16,256]{1,0:T(8,128)S(1)} %fusion.105), channel_id=1, replica_groups=mesh['layer'=2,'row'=4,'col'=4] {'col'}, use_global_device_ids=true, to_apply=%region_6.6 | all-reduce | flops 4096 | bytes 32768 | tf_op jit(solution)/shard_map/while/body/eval_jaxpr/psum | solution.py:44
  407.2 16.3 %psum.80 = f32[16,256]{1,0:T(8,128)S(1)} all-reduce(f32[16,256]{1,0:T(8,128)S(1)} %fusion.105), channel_id=1, replica_groups=mesh['layer'=2,'row'=4,'col'=4] {'col'}, use_global_device_ids=true, to_apply=%region_6.6 | all-reduce | flops 4096 | bytes 32768 | tf_op jit(solution)/shard_map/while/body/eval_jaxpr/psum | solution.py:44
  424.7 15.4 %psum.81 = f32[1,16,256]{2,1,0:T(8,128)S(1)} all-reduce(f32[1,16,256]{2,1,0:T(8,128)S(1)} %convolution_bitcast_fusion.5), channel_id=1, replica_groups=mesh['layer'=2,'row'=4,'col'=4] {'row'}, use_global_device_ids=true, to_apply=%region_7.7 | all-reduce | flops 4096 | bytes 32768 | tf_op jit(solution)/shard_map/while/body/eval_jaxpr/psum | solution.py:46
  443.5 15.6 %psum.80 = f32[16,256]{1,0:T(8,128)S(1)} all-reduce(f32[16,256]{1,0:T(8,128)S(1)} %fusion.105), channel_id=1, replica_groups=mesh['layer'=2,'row'=4,'col'=4] {'col'}, use_global_device_ids=true, to_apply=%region_6.6 | all-reduce | flops 4096 | bytes 32768 | tf_op jit(solution)/shard_map/while/body/eval_jaxpr/psum | solution.py:44
  477.4 16.3 %psum.80 = f32[16,256]{1,0:T(8,128)S(1)} all-reduce(f32[16,256]{1,0:T(8,128)S(1)} %fusion.105), channel_id=1, replica_groups=mesh['layer'=2,'row'=4,'col'=4] {'col'}, use_global_device_ids=true, to_apply=%region_6.6 | all-reduce | flops 4096 | bytes 32768 | tf_op jit(solution)/shard_map/while/body/eval_jaxpr/psum | solution.py:44
  494.9 15.4 %psum.81 = f32[1,16,256]{2,1,0:T(8,128)S(1)} all-reduce(f32[1,16,256]{2,1,0:T(8,128)S(1)} %convolution_bitcast_fusion.5), channel_id=1, replica_groups=mesh['layer'=2,'row'=4,'col'=4] {'row'}, use_global_device_ids=true, to_apply=%region_7.7 | all-reduce | flops 4096 | bytes 32768 | tf_op jit(solution)/shard_map/while/body/eval_jaxpr/psum | solution.py:46
  513.7 15.6 %psum.80 = f32[16,256]{1,0:T(8,128)S(1)} all-reduce(f32[16,256]{1,0:T(8,128)S(1)} %fusion.105), channel_id=1, replica_groups=mesh['layer'=2,'row'=4,'col'=4] {'col'}, use_global_device_ids=true, to_apply=%region_6.6 | all-reduce | flops 4096 | bytes 32768 | tf_op jit(solution)/shard_map/while/body/eval_jaxpr/psum | solution.py:44
  547.6 16.3 %psum.80 = f32[16,256]{1,0:T(8,128)S(1)} all-reduce(f32[16,256]{1,0:T(8,128)S(1)} %fusion.105), channel_id=1, replica_groups=mesh['layer'=2,'row'=4,'col'=4] {'col'}, use_global_device_ids=true, to_apply=%region_6.6 | all-reduce | flops 4096 | bytes 32768 | tf_op jit(solution)/shard_map/while/body/eval_jaxpr/psum | solution.py:44
  565.1 15.4 %psum.81 = f32[1,16,256]{2,1,0:T(8,128)S(1)} all-reduce(f32[1,16,256]{2,1,0:T(8,128)S(1)} %convolution_bitcast_fusion.5), channel_id=1, replica_groups=mesh['layer'=2,'row'=4,'col'=4] {'row'}, use_global_device_ids=true, to_apply=%region_7.7 | all-reduce | flops 4096 | bytes 32768 | tf_op jit(solution)/shard_map/while/body/eval_jaxpr/psum | solution.py:46
  583.9 15.6 %psum.80 = f32[16,256]{1,0:T(8,128)S(1)} all-reduce(f32[16,256]{1,0:T(8,128)S(1)} %fusion.105), channel_id=1, replica_groups=mesh['layer'=2,'row'=4,'col'=4] {'col'}, use_global_device_ids=true, to_apply=%region_6.6 | all-reduce | flops 4096 | bytes 32768 | tf_op jit(solution)/shard_map/while/body/eval_jaxpr/psum | solution.py:44
  614.5 215.2 %while.58 = (s32[]{:T(128)}, f32[8,16,256]{2,1,0:T(8,128)S(1)}, pred[]{:T(512)}, f32[8,16,256]{2,1,0:T(8,128)S(1)}, f32[8,8,256,256]{3,2,1,0:T(8,128)}, /*index=...) while((s32[]{:T(128)}, f32[8,16,256]{2,1,0:T(8,128)S(1)}, pred[]{:T(512)}, ...), condition=%wide.region_11.12_spmd, body=%wide.region_9.11_spmd.sunk | while | flops 113266696 | bytes 2819819 | solution.py:72
  845.8 222.6 %while.59 = (s32[]{:T(128)}, f32[8,32,256]{2,1,0:T(8,128)S(1)}, pred[]{:T(512)}, f32[8,32,256]{2,1,0:T(8,128)S(1)}, f32[8,32,256]{2,1,0:T(8,128)S(1)}, /*index=5...) while((s32[]{:T(128)}, f32[8,32,256]{2,1,0:T(8,128)S(1)}, ...), condition=%wide.region_14.15_spmd, body=%wide.region_12.14_spmd.sunk | while | flops 226541568 | bytes 3311347 | solution.py:72
  848.6 15.6 %psum.83 = f32[32,256]{1,0:T(8,128)S(1)} all-reduce(f32[32,256]{1,0:T(8,128)S(1)} %fusion.116), channel_id=1, replica_groups=mesh['layer'=2,'row'=4,'col'=4] {'row'}, use_global_device_ids=true, to_apply=%region_13.13 | all-reduce | flops 8192 | bytes 65536 | tf_op jit(solution)/shard_map/while/body/eval_jaxpr/psum | solution.py:67
  904.0 15.5 %psum.83 = f32[32,256]{1,0:T(8,128)S(1)} all-reduce(f32[32,256]{1,0:T(8,128)S(1)} %fusion.116), channel_id=1, replica_groups=mesh['layer'=2,'row'=4,'col'=4] {'row'}, use_global_device_ids=true, to_apply=%region_13.13 | all-reduce | flops 8192 | bytes 65536 | tf_op jit(solution)/shard_map/while/body/eval_jaxpr/psum | solution.py:67
  959.9 15.7 %psum.83 = f32[32,256]{1,0:T(8,128)S(1)} all-reduce(f32[32,256]{1,0:T(8,128)S(1)} %fusion.116), channel_id=1, replica_groups=mesh['layer'=2,'row'=4,'col'=4] {'row'}, use_global_device_ids=true, to_apply=%region_13.13 | all-reduce | flops 8192 | bytes 65536 | tf_op jit(solution)/shard_map/while/body/eval_jaxpr/psum | solution.py:67
  (213 shorter events, 602.3 us)
Async XLA Ops:
  7.2 323.2 %reduce-scatter.2.cloned.1.call-start = ((), (), s32[]{:S(2)}) async-start(), calls=%async_computation.1 | async-start | bytes 393216 | tf_op jit(solution)/shard_map/reduce_scatter | solution.py:91
  633.8 3.8 collective-permute-start
  637.6 4.6 collective-permute-start.1
  659.9 3.8 collective-permute-start
  663.7 4.6 collective-permute-start.1
  687.6 3.8 collective-permute-start
  691.4 4.6 collective-permute-start.1
  717.5 4.6 collective-permute-start.1
  741.3 3.8 collective-permute-start
  745.1 4.6 collective-permute-start.1
  767.4 3.8 collective-permute-start
  771.2 4.6 collective-permute-start.1
  795.1 3.8 collective-permute-start
  798.9 4.6 collective-permute-start.1
  821.2 3.8 collective-permute-start
  825.0 4.6 collective-permute-start.1
  865.5 4.0 collective-permute-start.2
  869.4 4.8 collective-permute-start.3
  892.4 4.0 collective-permute-start.2
  896.4 4.8 collective-permute-start.3
  920.7 4.0 collective-permute-start.2
  924.7 4.8 collective-permute-start.3
  948.3 4.0 collective-permute-start.2
  952.3 4.8 collective-permute-start.3
  976.8 4.0 collective-permute-start.2
  980.8 4.8 collective-permute-start.3
  1004.0 4.0 collective-permute-start.2
  1008.0 4.8 collective-permute-start.3
  1032.1 4.0 collective-permute-start.2
  1036.1 4.8 collective-permute-start.3
  1059.6 4.0 collective-permute-start.2
  1063.6 4.8 collective-permute-start.3
  (2 other events, 319.8 us)
Sparse Core Ops, SparseCore 0:
  323.2 7.0 reduce-scatter.1
